TPU v7x, 32 devices: a whole 2x2x4 slice. The times are simulated.
32 devices in a mesh: groups: 2 (over y), blk: 4 (over z), heads: 2 (over x), beam: 2 (over core).
Axes of the slice: x: 2, y: 2, z: 4, core: 2. Of those that a mesh axis runs over, the one named last changes fastest.
Arguments:
- queries: bfloat16 [4, 32, 64, 128], P(('groups', 'beam'), 'blk', 'heads'), parts along dimension 0, may hold values from -110 to 110
- positions: int32 [4, 32], P(('groups', 'beam'), 'blk'), parts along dimension 0, may hold values from 512 to 4096
- row_order: int32 [4, 32], P(('groups', 'beam')), parts along dimension 0, may hold values from 0 to 31, each once within a row
- lengths: int32 [8], P(('groups', 'blk')), parts along dimension 0, may hold values from 128 to 1024
- cache_keys: bfloat16 [8, 4, 1024, 128], P(('groups', 'blk'), 'heads'), parts along dimension 0, may hold values from -4 to 4
- cache_values: bfloat16 [8, 4, 1024, 128], P(('groups', 'blk'), 'heads'), parts along dimension 0, may hold values from -6 to 6
Outputs:
- attended: bfloat16 [4, 32, 64, 128], P(('groups', 'beam'), 'blk', 'heads'), parts along dimension 0
There are 2 independent parts, one for each index of `groups`. A program takes and returns all parts, laid end to end along the dimension named above; each array names one. Nothing has to cross between parts.
Inputs may be any that keep to these rules, and one draw needn't show every extreme that they name: Slots of shard s from lengths[s] on hold no cache entry. row_order[e] is a permutation of 0 to 31.
All inputs are finite; a program needn't handle non-finite values.
Results may differ from a plain program's by a relative error of at most 0.0015.
Values may be sent and summed in bfloat16 or wider, within the bound.
A program may use at most 64 MiB of HBM per device.

v0:
```python
import functools
import math

import jax
import jax.numpy as jnp
from jax import lax
from jax.experimental import pallas as pl
from jax.experimental.pallas import tpu as pltpu
from jax.sharding import PartitionSpec as P

KB = 256
MASKED = -1e30
FLOOR = -1e29
MESH = pl.DeviceIdType.MESH


def flipped(place, mask, bits):
    total = 0
    for bit in range(bits):
        digit = lax.rem(lax.div(place, 1 << bit), 2)
        total = total + lax.rem(digit + ((mask >> bit) & 1), 2) * (1 << bit)
    return total


def kernel(
    n, scale,
    pos_ref, order_ref, len_ref, q_hbm, k_hbm, v_hbm,
    out_ref,
    meta, q_all, k_buf, v_buf, vt_buf, sent, came,
    local_sem, relay_send, relay_recv, part_send, part_recv,
):
    me = lax.axis_index("blk")
    rows, kv, group, width = q_hbm.shape
    cap = k_hbm.shape[1]
    lanes = rows * group
    bits = n.bit_length() - 1

    q_in = [
        pltpu.make_async_copy(
            q_hbm.at[:, h], q_all[h].at[pl.ds(me * rows, rows)], local_sem.at[2 * kv + h]
        )
        for h in range(kv)
    ]
    k_in = [pltpu.make_async_copy(k_hbm.at[h], k_buf.at[h], local_sem.at[h]) for h in range(kv)]
    v_in = [pltpu.make_async_copy(v_hbm.at[h], v_buf.at[h], local_sem.at[kv + h]) for h in range(kv)]
    for copy in q_in + k_in + v_in:
        copy.start()

    for r in range(rows):
        meta[me, pl.ds(r, 1), :] = jnp.full((1, 128), pos_ref[0, r], jnp.int32)
    meta[me, pl.ds(rows, 1), :] = jnp.full((1, 128), len_ref[0], jnp.int32)

    barrier = pltpu.get_barrier_semaphore()
    has = {1: me + 1 < n, -1: me >= 1}
    for step in (1, -1):
        @pl.when(has[step])
        def _():
            pl.semaphore_signal(barrier, inc=1, device_id={"blk": me + step}, device_id_type=MESH)

    pl.semaphore_wait(barrier, has[1].astype(jnp.int32) + has[-1].astype(jnp.int32))

    def slot(item, source):
        if item == 0:
            return meta.at[source]
        return q_all[item - 1].at[pl.ds(source * rows, rows)]

    def relay(item, step, hops):
        way = 0 if step == 1 else 1
        block = slot(item, me - step * hops)
        return pltpu.make_async_remote_copy(
            src_ref=block, dst_ref=block,
            send_sem=relay_send.at[item, way, hops],
            recv_sem=relay_recv.at[item, way, hops + 1],
            device_id={"blk": me + step}, device_id_type=MESH,
        )

    def arrival(item, step, hops):
        way = 0 if step == 1 else 1
        block = slot(item, me - step * hops)
        return pltpu.make_async_remote_copy(
            src_ref=block, dst_ref=block,
            send_sem=relay_send.at[item, way, hops],
            recv_sem=relay_recv.at[item, way, hops],
            device_id={"blk": me - step}, device_id_type=MESH,
        )

    def begin(item):
        for step in (1, -1):
            @pl.when(has[step])
            def _():
                relay(item, step, 0).start()

    def turn(item, hops):
        for step in (1, -1):
            source = me - step * hops
            there = (source >= 0) & (source < n)

            @pl.when(there)
            def _():
                arrival(item, step, hops).wait_recv()

            @pl.when(there & has[step])
            def _():
                relay(item, step, hops).start()

    begin(0)
    for h in range(kv):
        q_in[h].wait()
        begin(1 + h)

    for h in range(kv):
        v_in[h].wait()
        vt_buf[h] = v_buf[h].astype(jnp.float32).T.astype(jnp.bfloat16)

    for hops in range(1, n):
        turn(0, hops)
        turn(1, hops)
        if hops == 1:
            for h in range(1, kv):
                turn(1 + h, hops)

    length = meta[me, pl.ds(rows, 1), :]
    offset = jnp.zeros((1, 128), jnp.int32)
    for s in range(n):
        offset = offset + jnp.where(s < me, meta[s, pl.ds(rows, 1), :], 0)
    lane_row = lax.broadcasted_iota(jnp.int32, (1, lanes), 1) // group
    slot_ids = lax.broadcasted_iota(jnp.int32, (KB, lanes), 0)

    def part(h, dest):
        pieces = []
        limit = jnp.zeros((1, lanes), jnp.int32)
        for r in range(rows):
            row = order_ref[0, dest * rows + r]
            pieces.append(q_all[h][row])
            limit = jnp.where(lane_row == r, meta[row // rows, pl.ds(row % rows, 1), :], limit)
        query = jnp.concatenate(pieces, axis=0)
        limit = jnp.minimum(length, limit - offset)
        outs, tots, tops = [], [], []
        for b in range(cap // KB):
            scores = lax.dot_general(
                k_buf[h, pl.ds(b * KB, KB), :], query, (((1,), (1,)), ((), ())),
                preferred_element_type=jnp.float32,
            )
            scores = jnp.where(slot_ids < limit - b * KB, scores, MASKED)
            top = jnp.max(scores, axis=0, keepdims=True)
            weights = jnp.exp2((scores - jnp.maximum(top, FLOOR)) * scale)
            tots.append(jnp.sum(weights, axis=0, keepdims=True))
            tops.append(top)
            outs.append(
                jnp.dot(
                    vt_buf[h, :, pl.ds(b * KB, KB)], weights.astype(jnp.bfloat16),
                    preferred_element_type=jnp.float32,
                )
            )
        return merge(outs, tots, tops)

    def merge(outs, tots, tops):
        best = functools.reduce(jnp.maximum, tops)
        out = tot = 0.0
        for o, t, p in zip(outs, tots, tops):
            factor = jnp.exp2((p - best) * scale)
            out = out + o * factor
            tot = tot + t * factor
        return out, tot, best

    def parcel(h, k):
        return pltpu.make_async_remote_copy(
            src_ref=sent.at[h, k], dst_ref=came.at[h, k],
            send_sem=part_send.at[h, k], recv_sem=part_recv.at[h, k],
            device_id={"blk": flipped(me, k, bits)}, device_id_type=MESH,
        )

    own = []
    for h in range(kv):
        k_in[h].wait()
        for k in range(n - 1, -1, -1):
            out, tot, top = part(h, flipped(me, k, bits))
            if k == 0:
                own.append((out, tot, top))
            else:
                sent[h, k, pl.ds(0, width), :] = out
                sent[h, k, pl.ds(width, 1), :] = tot
                sent[h, k, pl.ds(width + 1, 1), :] = top
                parcel(h, k).start()
            if h + 1 < kv and 2 <= n - k + 1 < n:
                turn(2 + h, n - k + 1)

    for h in range(kv):
        outs, tots, tops = ([x] for x in own[h])
        for k in range(n - 1, 0, -1):
            parcel(h, k).wait_recv()
            outs.append(came[h, k, pl.ds(0, width), :])
            tots.append(came[h, k, pl.ds(width, 1), :])
            tops.append(came[h, k, pl.ds(width + 1, 1), :])
        out, tot, _ = merge(outs, tots, tops)
        out_ref[:, h] = (out / tot).T.astype(jnp.bfloat16).reshape(rows, group, width)

    for h in range(kv):
        for k in range(n - 1, 0, -1):
            parcel(h, k).wait_send()
    for item in range(1 + kv):
        for hops in range(n - 1):
            for step in (1, -1):
                source = me - step * hops

                @pl.when((source >= 0) & (source < n) & has[step])
                def _():
                    relay(item, step, hops).wait_send()


def per_device(n, queries, positions, row_order, lengths, cache_keys, cache_values):
    keys, values = cache_keys[0], cache_values[0]
    kv, cap, width = keys.shape
    rows = queries.shape[1]
    group = queries.shape[2] // kv
    scale = float(width) ** -0.5 * math.log2(math.e)
    lanes = rows * group
    smem = pl.BlockSpec(memory_space=pltpu.SMEM)
    hbm = pl.BlockSpec(memory_space=pl.ANY)
    out = pl.pallas_call(
        functools.partial(kernel, n, scale),
        out_shape=jax.ShapeDtypeStruct((rows, kv, group, width), jnp.bfloat16),
        in_specs=[smem, smem, smem, hbm, hbm, hbm],
        out_specs=pl.BlockSpec(memory_space=pltpu.VMEM),
        scratch_shapes=[
            pltpu.VMEM((n, 2 * rows, 128), jnp.int32),
            [pltpu.VMEM((n * rows, group, width), jnp.bfloat16) for _ in range(kv)],
            pltpu.VMEM((kv, cap, width), jnp.bfloat16),
            pltpu.VMEM((kv, cap, width), jnp.bfloat16),
            pltpu.VMEM((kv, width, cap), jnp.bfloat16),
            pltpu.VMEM((kv, n, width + 8, lanes), jnp.float32),
            pltpu.VMEM((kv, n, width + 8, lanes), jnp.float32),
            pltpu.SemaphoreType.DMA((3 * kv,)),
            pltpu.SemaphoreType.DMA((1 + kv, 2, n)),
            pltpu.SemaphoreType.DMA((1 + kv, 2, n)),
            pltpu.SemaphoreType.DMA((kv, n)),
            pltpu.SemaphoreType.DMA((kv, n)),
        ],
        compiler_params=pltpu.CompilerParams(collective_id=0, has_side_effects=True),
        name="attend",
    )(
        positions, row_order, lengths,
        queries.reshape(rows, kv, group, width), keys, values,
    )
    return out.reshape(queries.shape)


def solution(mesh):
    placed = (
        P(("groups", "beam"), "blk", "heads", None),
        P(("groups", "beam"), "blk"),
        P(("groups", "beam"), None),
        P(("groups", "blk")),
        P(("groups", "blk"), "heads", None, None),
        P(("groups", "blk"), "heads", None, None),
    )
    return jax.shard_map(
        functools.partial(per_device, mesh.shape["blk"]),
        mesh=mesh,
        in_specs=placed,
        out_specs=P(("groups", "beam"), "blk", "heads", None),
        check_vma=False,
    )
```

profile of v0, /device:TPU:0, one launch (start us, length us, event | category | flops | bytes accessed | tf_op | source)
XLA Modules:
  0.0 27.6 jit_solution(15945232844951466681)
XLA Ops:
  0.7 25.5 %attend.1 = bf16[8,2,16,128]{3,2,1,0:T(8,128)(2,1)} custom-call(s32[1,8]{1,0:T(1,128)} %pos_ref.1, s32[1,32]{1,0:T(1,128)} %order_ref.1, s32[1]{0:T(128)S(6)} %copy.8.len_ref, bf16[8,2,16,128]{3,2,1,0:T(8,128)(2,1)} %bitcast.7, bf16[2,1024,128]{2,1,0:T(8,128)(2,1)} %bitcast.4, bf16[2,1024,128]{2,1,0:T(8,128)(2,1)} %bitcast.5), custom_call_target="tpu_custom_call" | custom-call | tf_op jit(solution)/shard_map/attend/pallas_call | solution.py:220
  26.2 1.5 %copy.9 = bf16[1,8,32,128]{3,2,1,0:T(8,128)(2,1)} copy(bf16[1,8,32,128]{3,2,1,0:T(8,128)(2,1)} %bitcast.6) | data formatting | bytes 131072
where the time goes:
time: 27.8 us; the launch traced here: 27.6 us
  Pallas kernels  25.5 us (92%)
  local copies, waits for them, and re-layouts  1.47 us (5%)
  between operations  0.66 us (2%)
    pallas_call x1, Pallas kernels, per_device(): pl.pallas_call(functools.partial(kernel, n, scale), out_shape=jax.ShapeDt...  25.5 us
    unnamed x1, local copies, waits for them, and re-layouts  1.47 us

commit v1 on v0

v1 whole, which is shorter than its diff:
```python
import functools
import math

import jax
import jax.numpy as jnp
from jax import lax
from jax.experimental import pallas as pl
from jax.experimental.pallas import tpu as pltpu
from jax.sharding import PartitionSpec as P

KB = 256
MASKED = -1e30
FLOOR = -1e29
STEPS = 32767.0
MESH = pl.DeviceIdType.MESH


def kernel(
    n, scale,
    pos_hbm, order_hbm, len_hbm, q_hbm, k_hbm, v_hbm,
    out_ref,
    pos_all, order, len_all, q_own, q_all, k_buf, v_buf, vt_buf, sent, came, sent_stat, came_stat,
    local_sem, pos_send, pos_recv, len_send, len_recv, order_send, order_recv, q_send, q_recv,
    part_send, part_recv, stat_send, stat_recv,
):
    me = lax.axis_index("blk")
    other = 1 - lax.axis_index("beam")
    rows, kv, group, width = q_hbm.shape
    cap = k_hbm.shape[1]
    lanes = rows * group

    q_in = [pltpu.make_async_copy(q_hbm.at[:, h], q_own.at[h], local_sem.at[h]) for h in range(kv)]
    k_in = [pltpu.make_async_copy(k_hbm.at[h], k_buf.at[h], local_sem.at[kv + h]) for h in range(kv)]
    v_in = [pltpu.make_async_copy(v_hbm.at[h], v_buf.at[h], local_sem.at[2 * kv + h]) for h in range(kv)]

    barrier = pltpu.get_barrier_semaphore()
    for d in range(n):
        pl.semaphore_signal(barrier, inc=1, device_id={"blk": d, "beam": other}, device_id_type=MESH)
    for copy in q_in + v_in + k_in:
        copy.start()

    def remote(src, dst, send, recv, d):
        return pltpu.make_async_remote_copy(
            src_ref=src, dst_ref=dst, send_sem=send, recv_sem=recv,
            device_id={"blk": d, "beam": other}, device_id_type=MESH,
        )

    def pos_copy(d, source):
        return remote(pos_hbm, pos_all.at[source], pos_send.at[d], pos_recv.at[source], d)

    def len_copy(d, source):
        return remote(len_hbm, len_all.at[source], len_send.at[d], len_recv.at[source], d)

    def order_copy():
        return remote(order_hbm, order, order_send, order_recv, me)

    def q_copy(h, d, source):
        return remote(
            q_own.at[h], q_all[h].at[pl.ds(source * rows, rows)],
            q_send.at[h, d], q_recv.at[h, source], d,
        )

    def parcel(h, d, source):
        return remote(
            sent.at[h, d], came.at[h, source],
            part_send.at[h, d], part_recv.at[h, source], d,
        )

    def stat(h, d, source):
        return remote(
            sent_stat.at[h, d], came_stat.at[h, source],
            stat_send.at[h, d], stat_recv.at[h, source], d,
        )

    for h in range(kv):
        q_in[h].wait()
    pl.semaphore_wait(barrier, n)
    for d in range(n - 1, -1, -1):
        pos_copy(d, me).start()
        len_copy(d, me).start()
    order_copy().start()
    for h in range(kv):
        for d in range(n - 1, -1, -1):
            q_copy(h, d, me).start()

    for h in range(kv):
        v_in[h].wait()
        vt_buf[h] = v_buf[h].astype(jnp.float32).T.astype(jnp.bfloat16)
        k_in[h].wait()

    order_copy().wait_recv()
    for s in range(n):
        pos_copy(s, s).wait_recv()
        len_copy(s, s).wait_recv()
    length = 0
    offset = 0
    for s in range(n):
        offset = offset + jnp.where(s < me, len_all[s, 0], 0)
        length = length + jnp.where(s == me, len_all[s, 0], 0)
    lane_row = lax.broadcasted_iota(jnp.int32, (1, lanes), 1) // group
    slot_ids = lax.broadcasted_iota(jnp.int32, (KB, lanes), 0)

    def part(h, d):
        pieces = []
        limit = jnp.zeros((1, lanes), jnp.int32)
        for r in range(rows):
            row = order[0, d * rows + r]
            pieces.append(q_all[h][row])
            limit = jnp.where(lane_row == r, pos_all[row // rows, 0, row % rows], limit)
        query = jnp.concatenate(pieces, axis=0)
        limit = jnp.minimum(length, limit - offset)
        outs, tots, tops = [], [], []
        for b in range(cap // KB):
            scores = lax.dot_general(
                k_buf[h, pl.ds(b * KB, KB), :], query, (((1,), (1,)), ((), ())),
                preferred_element_type=jnp.float32,
            )
            scores = jnp.where(slot_ids < limit - b * KB, scores, MASKED)
            top = jnp.max(scores, axis=0, keepdims=True)
            weights = jnp.exp2((scores - jnp.maximum(top, FLOOR)) * scale)
            tots.append(jnp.sum(weights, axis=0, keepdims=True))
            tops.append(top)
            outs.append(
                jnp.dot(
                    vt_buf[h, :, pl.ds(b * KB, KB)], weights.astype(jnp.bfloat16),
                    preferred_element_type=jnp.float32,
                )
            )
        return merge(outs, tots, tops)

    def merge(outs, tots, tops):
        best = functools.reduce(jnp.maximum, tops)
        out = tot = 0.0
        for o, t, p in zip(outs, tots, tops):
            factor = jnp.exp2((p - best) * scale)
            out = out + o * factor
            tot = tot + t * factor
        return out, tot, best

    for h in range(kv):
        for s in range(n):
            q_copy(h, s, s).wait_recv()
        for d in range(n):
            out, tot, top = part(h, d)
            largest = jnp.max(jnp.abs(out), axis=0, keepdims=True)
            unit = jnp.where(largest > 0.0, largest, 1.0)
            sent[h, d] = jnp.round(out * (STEPS / unit)).astype(jnp.int32).astype(jnp.int16)
            sent_stat[h, d, pl.ds(0, 1), :] = tot
            sent_stat[h, d, pl.ds(1, 1), :] = top
            sent_stat[h, d, pl.ds(2, 1), :] = unit * (1.0 / STEPS)
            parcel(h, d, me).start()
            stat(h, d, me).start()

    for h in range(kv):
        outs, tots, tops = [], [], []
        for s in range(n):
            stat(h, s, s).wait_recv()
            parcel(h, s, s).wait_recv()
            unit = came_stat[h, s, pl.ds(2, 1), :]
            outs.append(came[h, s].astype(jnp.int32).astype(jnp.float32) * unit)
            tots.append(came_stat[h, s, pl.ds(0, 1), :])
            tops.append(came_stat[h, s, pl.ds(1, 1), :])
        out, tot, _ = merge(outs, tots, tops)
        out_ref[:, h] = (out / tot).T.astype(jnp.bfloat16).reshape(rows, group, width)

    order_copy().wait_send()
    for d in range(n):
        pos_copy(d, me).wait_send()
        len_copy(d, me).wait_send()
        for h in range(kv):
            q_copy(h, d, me).wait_send()
            parcel(h, d, me).wait_send()
            stat(h, d, me).wait_send()


def per_device(n, queries, positions, row_order, lengths, cache_keys, cache_values):
    keys, values = cache_keys[0], cache_values[0]
    kv, cap, width = keys.shape
    rows = queries.shape[1]
    group = queries.shape[2] // kv
    scale = float(width) ** -0.5 * math.log2(math.e)
    lanes = rows * group
    hbm = pl.BlockSpec(memory_space=pltpu.HBM)
    dma = pltpu.SemaphoreType.DMA
    out = pl.pallas_call(
        functools.partial(kernel, n, scale),
        out_shape=pltpu.VMEM((rows, kv, group, width), jnp.bfloat16),
        in_specs=[hbm] * 6,
        out_specs=pl.BlockSpec(memory_space=pltpu.VMEM),
        scratch_shapes=[
            pltpu.SMEM((n, 1, rows), jnp.int32),
            pltpu.SMEM((1, n * rows), jnp.int32),
            pltpu.SMEM((n, 1), jnp.int32),
            pltpu.VMEM((kv, rows, group, width), jnp.bfloat16),
            [pltpu.VMEM((n * rows, group, width), jnp.bfloat16) for _ in range(kv)],
            pltpu.VMEM((kv, cap, width), jnp.bfloat16),
            pltpu.VMEM((kv, cap, width), jnp.bfloat16),
            pltpu.VMEM((kv, width, cap), jnp.bfloat16),
            pltpu.VMEM((kv, n, width, lanes), jnp.int16),
            pltpu.VMEM((kv, n, width, lanes), jnp.int16),
            pltpu.VMEM((kv, n, 8, lanes), jnp.float32),
            pltpu.VMEM((kv, n, 8, lanes), jnp.float32),
            dma((3 * kv,)),
            dma((n,)), dma((n,)), dma((n,)), dma((n,)), dma(()), dma(()),
            dma((kv, n)), dma((kv, n)), dma((kv, n)), dma((kv, n)), dma((kv, n)), dma((kv, n)),
        ],
        compiler_params=pltpu.CompilerParams(collective_id=0, has_side_effects=True),
        name="attend",
    )(
        positions, row_order, lengths,
        queries.reshape(rows, kv, group, width), keys, values,
    )
    return out.reshape(queries.shape)


def solution(mesh):
    placed = (
        P(("groups", "beam"), "blk", "heads", None),
        P(("groups", "beam"), "blk"),
        P(("groups", "beam"), None),
        P(("groups", "blk")),
        P(("groups", "blk"), "heads", None, None),
        P(("groups", "blk"), "heads", None, None),
    )
    return jax.shard_map(
        functools.partial(per_device, mesh.shape["blk"]),
        mesh=mesh,
        in_specs=placed,
        out_specs=P(("groups", "beam"), "blk", "heads", None),
        check_vma=False,
    )
```

time: 27.8 us -> 20.3 us (0.73)
  Pallas kernels: 25.5 us -> 18.8 us
  local copies, waits for them, and re-layouts: 1.47 us -> 0.63 us
    pallas_call x1, Pallas kernels: 25.5 us -> 18.8 us  [per_device(): pl.pallas_call(functools.partial(kernel, n, scale), out_shape=pltpu.VMEM(...]
    unnamed x1, local copies, waits for them, and re-layouts: 1.47 us -> 0.63 us
where the time goes in v1:
time: 20.3 us; the launch traced here: 20.1 us
  Pallas kernels  18.8 us (93%)
  between operations  0.66 us (3%)
  local copies, waits for them, and re-layouts  0.63 us (3%)
    pallas_call x1, Pallas kernels, per_device(): pl.pallas_call(functools.partial(kernel, n, scale), out_shape=pltpu.VMEM(...  18.8 us
    unnamed x1, local copies, waits for them, and re-layouts  0.63 us

profile of v1, /device:TPU:0, one launch (start us, length us, event | category | flops | bytes accessed | tf_op | source)
XLA Modules:
  0.0 20.1 jit_solution(12423621416789532241)
XLA Ops:
  0.7 18.8 %attend.1 = bf16[8,2,16,128]{3,2,1,0:T(8,128)(2,1)S(1)} custom-call(s32[1,8]{1,0:T(1,128)} %pos_hbm.1, s32[1,32]{1,0:T(1,128)} %order_hbm.1, s32[1]{0:T(128)S(6)} %copy.9.len_hbm, bf16[8,2,16,128]{3,2,1,0:T(8,128)(2,1)} %bitcast.7, bf16[2,1024,128]{2,1,0:T(8,128)(2,1)} %bitcast.5, bf16[2,1024,128]{2,1,0:T(8,128)(2,1)} %bitcast.6), custom_call_target="tpu_custom_call" | custom-call | tf_op jit(solution)/shard_map/attend/pallas_call | solution.py:185
  19.5 0.6 %copy.8 = bf16[1,8,32,128]{3,2,1,0:T(8,128)(2,1)} copy(bf16[1,8,32,128]{3,2,1,0:T(8,128)(2,1)S(1)} %bitcast.4) | data formatting | bytes 131072

commit v2 on v1

v2 whole, which is shorter than its diff:
```python
import functools
import math

import jax
import jax.numpy as jnp
from jax import lax
from jax.experimental import pallas as pl
from jax.experimental.pallas import tpu as pltpu
from jax.sharding import PartitionSpec as P

KB = 256
MASKED = -1e30
FLOOR = -1e29
STEPS = 32767.0
GROUP = 4
DELAY = 2
NEAREST = 1.5 * 2.0**23


def dest_order(n):
    return sorted(range(n), key=lambda d: d)


MESH = pl.DeviceIdType.MESH


def kernel(
    n, scale,
    pos_hbm, order_hbm, len_hbm, q_hbm, k_hbm, v_hbm,
    out_ref,
    pos_all, order, len_all, q_own, q_all, k_buf, v_buf, vt_buf, sent, came, sent_stat, came_stat,
    above, q_sem, kv_sem, meta_send, meta_recv, q_send, q_recv, part_send, part_recv, stat_send, stat_recv,
):
    me = lax.axis_index("blk")
    other = 1 - lax.axis_index("beam")
    rows, kv, group, width = q_hbm.shape
    cap = k_hbm.shape[1]
    lanes = rows * group

    q_in = pltpu.make_async_copy(q_hbm, q_own, q_sem)
    k_in = pltpu.make_async_copy(k_hbm, k_buf, kv_sem.at[0])
    v_in = pltpu.make_async_copy(v_hbm, v_buf, kv_sem.at[1])

    barrier = pltpu.get_barrier_semaphore()
    for d in range(n):
        @pl.when(d >= me)
        def _():
            pl.semaphore_signal(barrier, inc=1, device_id={"blk": d, "beam": other}, device_id_type=MESH)
    q_in.start()
    v_in.start()
    k_in.start()

    def remote(src, dst, send, recv, d):
        return pltpu.make_async_remote_copy(
            src_ref=src, dst_ref=dst, send_sem=send, recv_sem=recv,
            device_id={"blk": d, "beam": other}, device_id_type=MESH,
        )

    def pos_copy(d):
        return remote(pos_hbm, pos_all.at[me], meta_send.at[0], meta_recv.at[0], d)

    def len_copy(d):
        return remote(len_hbm, len_all.at[me], meta_send.at[1], meta_recv.at[1], d)

    def order_copy():
        return remote(order_hbm, order, meta_send.at[2], meta_recv.at[2], me)

    def q_copy(h, d):
        return remote(
            q_own.at[:, h], q_all[h].at[pl.ds(me * rows, rows)], q_send.at[h], q_recv.at[h], d
        )

    def parcel(h, d):
        return remote(sent.at[h, d], came.at[h, me], part_send.at[h], part_recv.at[h], d)

    def stat(h, d):
        return remote(sent_stat.at[h, d], came_stat.at[h, me], stat_send.at[h], stat_recv.at[h], d)

    def settle(ref, semaphore):
        pltpu.make_async_copy(ref, ref, semaphore).wait()

    def first_sends(d):
        pos_copy(d).start()
        len_copy(d).start()
        q_copy(0, d).start()

    pl.semaphore_wait(barrier, me + 1)
    for d in range(n - 1):
        @pl.when(d < me)
        def _():
            pl.semaphore_signal(above.at[me], inc=1, device_id={"blk": d, "beam": other}, device_id_type=MESH)
    q_in.wait()
    order_copy().start()
    for d in range(n):
        pl.when(d <= me)(functools.partial(first_sends, d))
    for step in range(1, n):
        @pl.when(me + step < n)
        def _():
            pl.semaphore_wait(above.at[me + step], 1)
            first_sends(me + step)
    v_in.wait()
    for h in range(kv):
        vt_buf[h] = v_buf[h].astype(jnp.float32).T.astype(jnp.bfloat16)
        if h + 1 < kv:
            pl.when(other == 0)(lambda: settle(q_all[h], q_send.at[h]))
            for d in range(n):
                q_copy(h + 1, d).start()
    k_in.wait()

    order_copy().wait_recv()
    settle(pos_all, meta_recv.at[0])
    settle(len_all, meta_recv.at[1])
    length = 0
    offset = 0
    for s in range(n):
        offset = offset + jnp.where(s < me, len_all[s, 0], 0)
        length = length + jnp.where(s == me, len_all[s, 0], 0)
    lane_row = lax.broadcasted_iota(jnp.int32, (1, lanes), 1) // group
    slot_ids = lax.broadcasted_iota(jnp.int32, (KB, lanes), 0)

    blocks = cap // KB

    def gather(h, d):
        pieces = []
        limit = jnp.zeros((1, lanes), jnp.int32)
        for r in range(rows):
            row = order[0, d * rows + r]
            pieces.append(q_all[h][row])
            limit = jnp.where(lane_row == r, pos_all[row // rows, 0, row % rows], limit)
        return jnp.concatenate(pieces, axis=0), jnp.minimum(length, limit - offset)

    def dot(h, query, b):
        return lax.dot_general(
            k_buf[h, pl.ds(b * KB, KB), :], query, (((1,), (1,)), ((), ())),
            preferred_element_type=jnp.float32,
        )

    def finish(h, d, outs, tots, tops):
        best = functools.reduce(jnp.maximum, tops)
        out = tot = 0.0
        for o, t, p in zip(outs, tots, tops):
            factor = jnp.exp2((p - best) * scale)
            out = out + o * factor
            tot = tot + t * factor
        largest = jnp.max(jnp.abs(out), axis=0, keepdims=True)
        unit = jnp.where(largest > 0.0, largest, 1.0)
        sent[h, d] = (out * (STEPS / unit) + NEAREST - NEAREST).astype(jnp.int32).astype(jnp.int16)
        sent_stat[h, d, pl.ds(0, 1), :] = tot
        sent_stat[h, d, pl.ds(1, 1), :] = best
        sent_stat[h, d, pl.ds(2, 1), :] = unit * (1.0 / STEPS)

    def parts(h, dests):
        fetched = [gather(h, d) for d in dests]
        steps = [(i, b) for i in range(len(dests)) for b in range(blocks)]
        ahead = dot(h, fetched[0][0], 0)
        done = ready = None
        for at, (i, b) in enumerate(steps):
            query, limit = fetched[i]
            if b == 0:
                outs, tots, tops = [], [], []
            scores = jnp.where(slot_ids < limit - b * KB, ahead, MASKED)
            if at + 1 < len(steps):
                j, c = steps[at + 1]
                ahead = dot(h, fetched[j][0], c)
            top = jnp.max(scores, axis=0, keepdims=True)
            weights = jnp.exp2((scores - jnp.maximum(top, FLOOR)) * scale)
            tots.append(jnp.sum(weights, axis=0, keepdims=True))
            tops.append(top)
            outs.append(
                jnp.dot(
                    vt_buf[h, :, pl.ds(b * KB, KB)], weights.astype(jnp.bfloat16),
                    preferred_element_type=jnp.float32,
                )
            )
            if done is not None and b == 0:
                finish(h, *done)
                ready = done[0]
                done = None
            if ready is not None and b == DELAY:
                parcel(h, ready).start()
                stat(h, ready).start()
                ready = None
            if b + 1 == blocks:
                done = (dests[i], outs, tots, tops)
        finish(h, *done)
        parcel(h, done[0]).start()
        stat(h, done[0]).start()

    for h in range(kv):
        settle(q_all[h], q_recv.at[h])
        ordered = dest_order(n)
        for i in range(0, n, GROUP):
            dests = ordered[i:i + GROUP]
            parts(h, dests)

    settle(pos_all, meta_send.at[0])
    settle(len_all, meta_send.at[1])
    order_copy().wait_send()
    settle(q_all[kv - 1], q_send.at[kv - 1])
    for h in range(kv - 1):
        pl.when(other == 1)(lambda: settle(q_all[h], q_send.at[h]))

    for h in range(kv):
        settle(came_stat.at[h], stat_recv.at[h])
        tops = [came_stat[h, s, pl.ds(1, 1), :] for s in range(n)]
        best = functools.reduce(jnp.maximum, tops)
        factors = [jnp.exp2((p - best) * scale) for p in tops]
        tot = sum(came_stat[h, s, pl.ds(0, 1), :] * factors[s] for s in range(n))
        inverse = 1.0 / tot
        settle(came.at[h], part_recv.at[h])
        out = 0.0
        for s in range(n):
            factor = came_stat[h, s, pl.ds(2, 1), :] * factors[s] * inverse
            out = out + came[h, s].astype(jnp.int32).astype(jnp.float32) * factor
        out_ref[:, h] = out.T.astype(jnp.bfloat16).reshape(rows, group, width)

    for h in range(kv):
        settle(sent.at[h], part_send.at[h])
        settle(sent_stat.at[h], stat_send.at[h])


def per_device(n, queries, positions, row_order, lengths, cache_keys, cache_values):
    keys, values = cache_keys[0], cache_values[0]
    kv, cap, width = keys.shape
    rows = queries.shape[1]
    group = queries.shape[2] // kv
    scale = float(width) ** -0.5 * math.log2(math.e)
    lanes = rows * group
    hbm = pl.BlockSpec(memory_space=pltpu.HBM)
    dma = pltpu.SemaphoreType.DMA
    out = pl.pallas_call(
        functools.partial(kernel, n, scale),
        out_shape=pltpu.VMEM((rows, kv, group, width), jnp.bfloat16),
        in_specs=[hbm] * 6,
        out_specs=pl.BlockSpec(memory_space=pltpu.VMEM),
        scratch_shapes=[
            pltpu.SMEM((n, 1, rows), jnp.int32),
            pltpu.SMEM((1, n * rows), jnp.int32),
            pltpu.SMEM((n, 1), jnp.int32),
            pltpu.VMEM((rows, kv, group, width), jnp.bfloat16),
            [pltpu.VMEM((n * rows, group, width), jnp.bfloat16) for _ in range(kv)],
            pltpu.VMEM((kv, cap, width), jnp.bfloat16),
            pltpu.VMEM((kv, cap, width), jnp.bfloat16),
            pltpu.VMEM((kv, width, cap), jnp.bfloat16),
            pltpu.VMEM((kv, n, width, lanes), jnp.int16),
            pltpu.VMEM((kv, n, width, lanes), jnp.int16),
            pltpu.VMEM((kv, n, 3, lanes), jnp.float32),
            pltpu.VMEM((kv, n, 3, lanes), jnp.float32),
            pltpu.SemaphoreType.REGULAR((n,)),
            dma(()), dma((2,)), dma((3,)), dma((3,)),
            dma((kv,)), dma((kv,)), dma((kv,)), dma((kv,)), dma((kv,)), dma((kv,)),
        ],
        compiler_params=pltpu.CompilerParams(collective_id=0, has_side_effects=True),
        name="attend",
    )(
        positions, row_order, lengths,
        queries.reshape(rows, kv, group, width), keys, values,
    )
    return out.reshape(queries.shape)


def solution(mesh):
    placed = (
        P(("groups", "beam"), "blk", "heads", None),
        P(("groups", "beam"), "blk"),
        P(("groups", "beam"), None),
        P(("groups", "blk")),
        P(("groups", "blk"), "heads", None, None),
        P(("groups", "blk"), "heads", None, None),
    )
    return jax.shard_map(
        functools.partial(per_device, mesh.shape["blk"]),
        mesh=mesh,
        in_specs=placed,
        out_specs=P(("groups", "beam"), "blk", "heads", None),
        check_vma=False,
    )
```

time: 20.3 us -> 18.1 us (0.89)
  Pallas kernels: 18.8 us -> 16.5 us
    pallas_call x1, Pallas kernels: 18.8 us -> 16.5 us  [per_device(): pl.pallas_call(functools.partial(kernel, n, scale), out_shape=pltpu.VMEM(...]
where the time goes in v2:
time: 18.1 us; the launch traced here: 17.8 us
  Pallas kernels  16.5 us (91%)
  between operations  0.66 us (4%)
  local copies, waits for them, and re-layouts  0.63 us (3%)
    pallas_call x1, Pallas kernels, per_device(): pl.pallas_call(functools.partial(kernel, n, scale), out_shape=pltpu.VMEM(...  16.5 us
    unnamed x1, local copies, waits for them, and re-layouts  0.63 us

profile of v2, /device:TPU:0, one launch (start us, length us, event | category | flops | bytes accessed | tf_op | source)
XLA Modules:
  0.0 17.8 jit_solution(3576822380146815809)
XLA Ops:
  0.7 16.5 %attend.1 = bf16[8,2,16,128]{3,2,1,0:T(8,128)(2,1)S(1)} custom-call(s32[1,8]{1,0:T(1,128)} %pos_hbm.1, s32[1,32]{1,0:T(1,128)} %order_hbm.1, s32[1]{0:T(128)S(6)} %copy.9.len_hbm, bf16[8,2,16,128]{3,2,1,0:T(8,128)(2,1)} %bitcast.7, bf16[2,1024,128]{2,1,0:T(8,128)(2,1)} %bitcast.5, bf16[2,1024,128]{2,1,0:T(8,128)(2,1)} %bitcast.6), custom_call_target="tpu_custom_call" | custom-call | tf_op jit(solution)/shard_map/attend/pallas_call | solution.py:231
  17.1 0.6 %copy.8 = bf16[1,8,32,128]{3,2,1,0:T(8,128)(2,1)} copy(bf16[1,8,32,128]{3,2,1,0:T(8,128)(2,1)S(1)} %bitcast.4) | data formatting | bytes 131072

commit v3 on v2

--- a/solution.py
+++ b/solution.py
@@ -12,7 +12,7 @@
 MASKED = -1e30
 FLOOR = -1e29
 STEPS = 32767.0
-GROUP = 4
+GROUP = 2
 DELAY = 2
 NEAREST = 1.5 * 2.0**23
 
@@ -29,7 +29,7 @@
     pos_hbm, order_hbm, len_hbm, q_hbm, k_hbm, v_hbm,
     out_ref,
     pos_all, order, len_all, q_own, q_all, k_buf, v_buf, vt_buf, sent, came, sent_stat, came_stat,
-    above, q_sem, kv_sem, meta_send, meta_recv, q_send, q_recv, part_send, part_recv, stat_send, stat_recv,
+    above, q_sem, kv_sem, meta_send, meta_recv, q_send, q_recv, pass_send, part_send, part_recv, stat_send, stat_recv,
 ):
     me = lax.axis_index("blk")
     other = 1 - lax.axis_index("beam")
@@ -37,16 +37,27 @@
     cap = k_hbm.shape[1]
     lanes = rows * group
 
-    q_in = pltpu.make_async_copy(q_hbm, q_own, q_sem)
+    q_in = [pltpu.make_async_copy(q_hbm.at[r], q_own.at[r], q_sem) for r in range(rows)]
     k_in = pltpu.make_async_copy(k_hbm, k_buf, kv_sem.at[0])
     v_in = pltpu.make_async_copy(v_hbm, v_buf, kv_sem.at[1])
 
+    folded = n > 2 and n % 2 == 0
+    odd = lax.rem(me, 2)
+    passer = (odd == 0) & (me > 0)
+    passed = (odd == 1) & (me < n - 1)
+    beside = {"blk": jnp.where(odd == 1, me - 1, me + 1)}
+
     barrier = pltpu.get_barrier_semaphore()
     for d in range(n):
-        @pl.when(d >= me)
+        @pl.when((d > me) | ((d == me) & (other == 0)))
         def _():
             pl.semaphore_signal(barrier, inc=1, device_id={"blk": d, "beam": other}, device_id_type=MESH)
-    q_in.start()
+    if folded:
+        @pl.when(passer)
+        def _():
+            pl.semaphore_signal(barrier, inc=1, device_id=beside, device_id_type=MESH)
+    for copy in q_in:
+        copy.start()
     v_in.start()
     k_in.start()
 
@@ -66,9 +77,42 @@
         return remote(order_hbm, order, meta_send.at[2], meta_recv.at[2], me)
 
     def q_copy(h, d):
+        onward = jnp.where((d == me + 1) & passed, 1, 0) if folded else 0
         return remote(
-            q_own.at[:, h], q_all[h].at[pl.ds(me * rows, rows)], q_send.at[h], q_recv.at[h], d
+            q_own.at[:, h], q_all[h].at[pl.ds(me * rows, rows)], q_send.at[h], q_recv.at[onward, h], d
         )
+
+    def send_q(h, d):
+        if folded:
+            pl.when(jnp.logical_not((d == me + 2) & passed))(lambda: q_copy(h, d).start())
+        else:
+            q_copy(h, d).start()
+
+    def pass_copy(h):
+        slot = q_all[h].at[pl.ds((me - 1) * rows, rows)]
+        return pltpu.make_async_remote_copy(
+            src_ref=slot, dst_ref=slot, send_sem=pass_send.at[h], recv_sem=q_recv.at[0, h],
+            device_id=beside, device_id_type=MESH,
+        )
+
+    def pass_q(h):
+        if folded:
+            @pl.when(passer)
+            def _():
+                settle(q_all[h].at[pl.ds(0, rows)], q_recv.at[1, h])
+                pass_copy(h).start()
+
+    def settle_q(h, semaphore, fewer):
+        if folded:
+            @pl.when(fewer)
+            def _():
+                settle(q_all[h].at[pl.ds(0, (n - 1) * rows)], semaphore)
+
+            @pl.when(jnp.logical_not(fewer))
+            def _():
+                settle(q_all[h], semaphore)
+        else:
+            settle(q_all[h], semaphore)
 
     def parcel(h, d):
         return remote(sent.at[h, d], came.at[h, me], part_send.at[h], part_recv.at[h], d)
@@ -82,29 +126,49 @@
     def first_sends(d):
         pos_copy(d).start()
         len_copy(d).start()
-        q_copy(0, d).start()
-
-    pl.semaphore_wait(barrier, me + 1)
+        send_q(0, d)
+
+    greeted = me + other
+    if folded:
+        greeted = greeted + jnp.where((odd == 1) & (me > 1), 1, 0)
+
+    @pl.when(greeted > 0)
+    def _():
+        pl.semaphore_wait(barrier, greeted)
+
+    for d in range(n):
+        @pl.when((d < me) | ((d == me) & (other == 1)))
+        def _():
+            pl.semaphore_signal(above.at[me], inc=1, device_id={"blk": d, "beam": other}, device_id_type=MESH)
+    if folded:
+        @pl.when((odd == 1) & (me > 1))
+        def _():
+            pl.semaphore_signal(above.at[n], inc=1, device_id=beside, device_id_type=MESH)
+    settle(q_own, q_sem)
+    for d in range(n - 2, -1, -1):
+        pl.when((d < me) & (other == 1))(functools.partial(first_sends, d))
     for d in range(n - 1):
-        @pl.when(d < me)
-        def _():
-            pl.semaphore_signal(above.at[me], inc=1, device_id={"blk": d, "beam": other}, device_id_type=MESH)
-    q_in.wait()
+        pl.when((d < me) & (other == 0))(functools.partial(first_sends, d))
+    pl.when(other == 0)(lambda: pl.semaphore_wait(above.at[me], 1))
     order_copy().start()
-    for d in range(n):
-        pl.when(d <= me)(functools.partial(first_sends, d))
+    first_sends(me)
     for step in range(1, n):
         @pl.when(me + step < n)
         def _():
             pl.semaphore_wait(above.at[me + step], 1)
             first_sends(me + step)
+            if step == 1 and folded:
+                for h in range(1, kv):
+                    pl.when(passed)(functools.partial(send_q, h, me + step))
     v_in.wait()
     for h in range(kv):
         vt_buf[h] = v_buf[h].astype(jnp.float32).T.astype(jnp.bfloat16)
         if h + 1 < kv:
-            pl.when(other == 0)(lambda: settle(q_all[h], q_send.at[h]))
+            pl.when(other == 0)(lambda: settle_q(h, q_send.at[h], passed))
             for d in range(n):
-                q_copy(h + 1, d).start()
+                pl.when((d > me) & jnp.logical_not(passed & (d == me + 1)))(functools.partial(send_q, h + 1, d))
+            for d in range(n):
+                pl.when(d <= me)(functools.partial(send_q, h + 1, d))
     k_in.wait()
 
     order_copy().wait_recv()
@@ -186,9 +250,14 @@
         parcel(h, done[0]).start()
         stat(h, done[0]).start()
 
+    if folded:
+        pl.when(passer)(lambda: pl.semaphore_wait(above.at[n], 1))
+    pass_q(0)
     for h in range(kv):
-        settle(q_all[h], q_recv.at[h])
+        settle_q(h, q_recv.at[0, h], passer)
         ordered = dest_order(n)
+        if h + 1 < kv:
+            pass_q(h + 1)
         for i in range(0, n, GROUP):
             dests = ordered[i:i + GROUP]
             parts(h, dests)
@@ -196,9 +265,14 @@
     settle(pos_all, meta_send.at[0])
     settle(len_all, meta_send.at[1])
     order_copy().wait_send()
-    settle(q_all[kv - 1], q_send.at[kv - 1])
+    settle_q(kv - 1, q_send.at[kv - 1], passed)
     for h in range(kv - 1):
-        pl.when(other == 1)(lambda: settle(q_all[h], q_send.at[h]))
+        pl.when(other == 1)(lambda: settle_q(h, q_send.at[h], passed))
+    if folded:
+        @pl.when(passer)
+        def _():
+            for h in range(kv):
+                pass_copy(h).wait_send()
 
     for h in range(kv):
         settle(came_stat.at[h], stat_recv.at[h])
@@ -246,9 +320,9 @@
             pltpu.VMEM((kv, n, width, lanes), jnp.int16),
             pltpu.VMEM((kv, n, 3, lanes), jnp.float32),
             pltpu.VMEM((kv, n, 3, lanes), jnp.float32),
-            pltpu.SemaphoreType.REGULAR((n,)),
+            pltpu.SemaphoreType.REGULAR((n + 1,)),
             dma(()), dma((2,)), dma((3,)), dma((3,)),
-            dma((kv,)), dma((kv,)), dma((kv,)), dma((kv,)), dma((kv,)), dma((kv,)),
+            dma((kv,)), dma((2, kv)), dma((kv,)), dma((kv,)), dma((kv,)), dma((kv,)), dma((kv,)),
         ],
         compiler_params=pltpu.CompilerParams(collective_id=0, has_side_effects=True),
         name="attend",

time: 18.1 us -> 18.1 us (level)
  the two profiles are of different devices: /device:TPU:0 before, /device:TPU:1 now
where the time goes in v3:
time: 18.1 us; the launch traced here: 17.9 us
  Pallas kernels  16.6 us (92%)
  between operations  0.66 us (4%)
  local copies, waits for them, and re-layouts  0.63 us (3%)
    pallas_call x1, Pallas kernels, per_device(): pl.pallas_call(functools.partial(kernel, n, scale), out_shape=pltpu.VMEM(...  16.6 us
    unnamed x1, local copies, waits for them, and re-layouts  0.63 us

profile of v3, /device:TPU:1, one launch (start us, length us, event | category | flops | bytes accessed | tf_op | source)
XLA Modules:
  0.0 17.9 jit_solution(10802128776671861407)
XLA Ops:
  0.7 16.6 %attend.1 = bf16[8,2,16,128]{3,2,1,0:T(8,128)(2,1)S(1)} custom-call(s32[1,8]{1,0:T(1,128)} %pos_hbm.1, s32[1,32]{1,0:T(1,128)} %order_hbm.1, s32[1]{0:T(128)S(6)} %copy.9.len_hbm, bf16[8,2,16,128]{3,2,1,0:T(8,128)(2,1)} %bitcast.7, bf16[2,1024,128]{2,1,0:T(8,128)(2,1)} %bitcast.5, bf16[2,1024,128]{2,1,0:T(8,128)(2,1)} %bitcast.6), custom_call_target="tpu_custom_call" | custom-call | tf_op jit(solution)/shard_map/attend/pallas_call | solution.py:305
  17.3 0.6 %copy.8 = bf16[1,8,32,128]{3,2,1,0:T(8,128)(2,1)} copy(bf16[1,8,32,128]{3,2,1,0:T(8,128)(2,1)S(1)} %bitcast.4) | data formatting | bytes 131072

commit v4 on v2

--- a/solution.py
+++ b/solution.py
@@ -91,7 +91,7 @@
             pl.semaphore_signal(above.at[me], inc=1, device_id={"blk": d, "beam": other}, device_id_type=MESH)
     q_in.wait()
     order_copy().start()
-    for d in range(n):
+    for d in range(n - 1, -1, -1):
         pl.when(d <= me)(functools.partial(first_sends, d))
     for step in range(1, n):
         @pl.when(me + step < n)
@@ -103,7 +103,7 @@
         vt_buf[h] = v_buf[h].astype(jnp.float32).T.astype(jnp.bfloat16)
         if h + 1 < kv:
             pl.when(other == 0)(lambda: settle(q_all[h], q_send.at[h]))
-            for d in range(n):
+            for d in (*range(1, n), 0):
                 q_copy(h + 1, d).start()
     k_in.wait()
 

time: 18.1 us -> 18.1 us (level)
  no operation moved by 1% of the time
where the time goes in v4:
time: 18.1 us; the launch traced here: 17.8 us
  Pallas kernels  16.5 us (91%)
  between operations  0.66 us (4%)
  local copies, waits for them, and re-layouts  0.63 us (3%)
    pallas_call x1, Pallas kernels, per_device(): pl.pallas_call(functools.partial(kernel, n, scale), out_shape=pltpu.VMEM(...  16.5 us
    unnamed x1, local copies, waits for them, and re-layouts  0.63 us

profile of v4, /device:TPU:0, one launch (start us, length us, event | category | flops | bytes accessed | tf_op | source)
XLA Modules:
  0.0 17.8 jit_solution(12287157547101260468)
XLA Ops:
  0.7 16.5 %attend.1 = bf16[8,2,16,128]{3,2,1,0:T(8,128)(2,1)S(1)} custom-call(s32[1,8]{1,0:T(1,128)} %pos_hbm.1, s32[1,32]{1,0:T(1,128)} %order_hbm.1, s32[1]{0:T(128)S(6)} %copy.9.len_hbm, bf16[8,2,16,128]{3,2,1,0:T(8,128)(2,1)} %bitcast.7, bf16[2,1024,128]{2,1,0:T(8,128)(2,1)} %bitcast.5, bf16[2,1024,128]{2,1,0:T(8,128)(2,1)} %bitcast.6), custom_call_target="tpu_custom_call" | custom-call | tf_op jit(solution)/shard_map/attend/pallas_call | solution.py:231
  17.2 0.6 %copy.8 = bf16[1,8,32,128]{3,2,1,0:T(8,128)(2,1)} copy(bf16[1,8,32,128]{3,2,1,0:T(8,128)(2,1)S(1)} %bitcast.4) | data formatting | bytes 131072

commit v5 on v4

--- a/solution.py
+++ b/solution.py
@@ -189,6 +189,8 @@
     for h in range(kv):
         settle(q_all[h], q_recv.at[h])
         ordered = dest_order(n)
+        if h > 0:
+            ordered = sorted(ordered, key=lambda d: min(d, n - 1 - d))
         for i in range(0, n, GROUP):
             dests = ordered[i:i + GROUP]
             parts(h, dests)

time: 18.1 us -> 18 us (level)
  no operation moved by 1% of the time
where the time goes in v5:
time: 18 us; the launch traced here: 17.8 us
  Pallas kernels  16.5 us (92%)
  between operations  0.66 us (4%)
  local copies, waits for them, and re-layouts  0.63 us (4%)
    pallas_call x1, Pallas kernels, per_device(): pl.pallas_call(functools.partial(kernel, n, scale), out_shape=pltpu.VMEM(...  16.5 us
    unnamed x1, local copies, waits for them, and re-layouts  0.63 us

profile of v5, /device:TPU:0, one launch (start us, length us, event | category | flops | bytes accessed | tf_op | source)
XLA Modules:
  0.0 17.8 jit_solution(18029754739866718700)
XLA Ops:
  0.7 16.5 %attend.1 = bf16[8,2,16,128]{3,2,1,0:T(8,128)(2,1)S(1)} custom-call(s32[1,8]{1,0:T(1,128)} %pos_hbm.1, s32[1,32]{1,0:T(1,128)} %order_hbm.1, s32[1]{0:T(128)S(6)} %copy.9.len_hbm, bf16[8,2,16,128]{3,2,1,0:T(8,128)(2,1)} %bitcast.7, bf16[2,1024,128]{2,1,0:T(8,128)(2,1)} %bitcast.5, bf16[2,1024,128]{2,1,0:T(8,128)(2,1)} %bitcast.6), custom_call_target="tpu_custom_call" | custom-call | tf_op jit(solution)/shard_map/attend/pallas_call | solution.py:233
  17.2 0.6 %copy.8 = bf16[1,8,32,128]{3,2,1,0:T(8,128)(2,1)} copy(bf16[1,8,32,128]{3,2,1,0:T(8,128)(2,1)S(1)} %bitcast.4) | data formatting | bytes 131072
